TPU v7x, 32 devices: a whole 2x2x4 slice. The times are simulated.
32 devices in a mesh: cells: 8 (over y, x, core), genes: 4 (over z).
Axes of the slice: x: 2, y: 2, z: 4, core: 2. Of those that a mesh axis runs over, the one named last changes fastest.
Arguments:
- counts: int32 [8192, 4096], P('cells', 'genes'), may hold values from 0 to 26, as said below
- library: int32 [8192], P('cells'), may hold values from 2000 to 19999
Outputs:
- adjacency: float32 [4096, 4096], P('cells', 'genes')
- connectivity: float32 [4096], P('cells')
Inputs may be any that keep to these rules, and one draw needn't show every extreme that they name: Non-negative integer counts.
All inputs are finite; a program needn't handle non-finite values.
Results may differ from a plain program's by a relative error of at most 0.006.
Values may be sent and summed in bfloat16 or wider, within the bound.
A program may use at most 128 MiB of HBM per device.

v0:
```python
import jax
import jax.numpy as jnp
from jax import lax
from jax.sharding import PartitionSpec as P


def normalize(counts, library):
    factor = 10000.0 / library.astype(jnp.float32)
    return jnp.log1p(counts.astype(jnp.float32) * factor[:, None]).astype(jnp.bfloat16)


def cross_product(left, right):
    return lax.dot_general(
        left, right, (((0,), (0,)), ((), ())), preferred_element_type=jnp.float32
    )


def shards(counts, library):
    own_block = normalize(counts, library)
    col_width = own_block.shape[1]
    cell_groups = lax.axis_size("cells")
    gene_total = col_width * lax.axis_size("genes")
    row_width = gene_total // cell_groups
    total_cells = float(counts.shape[0] * cell_groups)
    widened = own_block.astype(jnp.float32)
    local_sums = jnp.sum(widened, axis=0)
    local_squares = jnp.sum(widened * widened, axis=0)
    block_sums, block_squares = lax.psum((local_sums, local_squares), "cells")
    gene_sums, gene_squares = (
        lax.all_gather(block_sums, "genes", axis=0, tiled=True),
        lax.all_gather(block_squares, "genes", axis=0, tiled=True),
    )
    full_block = lax.all_gather(own_block, "genes", axis=1, tiled=True)
    gram_tile = lax.psum_scatter(
        cross_product(full_block, own_block), "cells", scatter_dimension=0, tiled=True
    )
    means = gene_sums / total_cells
    variances = gene_squares / total_cells - means * means
    scales = lax.rsqrt(variances + 1e-05)
    row_first = lax.axis_index("cells") * row_width
    col_first = lax.axis_index("genes") * col_width
    row_means = lax.dynamic_slice_in_dim(means, row_first, row_width, 0)
    col_means = lax.dynamic_slice_in_dim(means, col_first, col_width, 0)
    row_scales = lax.dynamic_slice_in_dim(scales, row_first, row_width, 0)
    col_scales = lax.dynamic_slice_in_dim(scales, col_first, col_width, 0)
    correlation = (
        (gram_tile / total_cells - row_means[:, None] * col_means[None, :])
        * row_scales[:, None]
        * col_scales[None, :]
    )
    powered = correlation**6
    row_index = row_first + jnp.arange(row_width, dtype=jnp.int32)[:, None]
    col_index = col_first + jnp.arange(col_width, dtype=jnp.int32)[None, :]
    adjacency = jnp.where(row_index == col_index, jnp.float32(0.0), powered)
    connectivity = lax.psum(jnp.sum(adjacency, axis=1), "genes")
    return (adjacency, connectivity)


def solution(mesh):
    return jax.shard_map(
        shards,
        mesh=mesh,
        in_specs=(P("cells", "genes"), P("cells")),
        out_specs=(P("cells", "genes"), P("cells")),
        check_vma=False,
    )
```

profile of v0, /device:TPU:0, one launch (start us, length us, event | category | flops | bytes accessed | tf_op | source)
XLA Modules:
  0.0 318.0 jit_solution(6613592547870994486)
XLA Ops:
  7.2 0.0 all-gather.2.cloned.1.call-start
  7.2 0.7 convert_divide_fusion
  7.9 5.6 %convert_reduce_fusion = (f32[1024]{0:T(1024)S(1)}, f32[1024]{0:T(1024)S(1)}, bf16[1024,1024]{1,0:T(8,128)(2,1)}) fusion(f32[1024]{0:T(1024)S(1)} %convert_divide_fusion, s32[1024,1024]{1,0:T(8,128)} %param.2), kind=kLoop, calls=%fused_computation.1 | loop fusion | flops 7337984 | bytes 6303744 | tf_op jit(solution)/shard_map/reduce_sum | solution.py:26
  13.5 0.0 copy-start
  13.5 0.0 all-gather.2.cloned.1.call-update
  13.5 0.0 reduce-scatter.2.cloned.1.call-start
  13.5 152.4 %all-gather.2.cloned.1.call-done = bf16[1024,4096]{1,0:T(8,128)(2,1)} async-done(((bf16[1024,1024]{1,0:T(8,128)(2,1)}), bf16[1024,4096]{1,0:T(8,128)(2,1)}) %all-gather.2.cloned.1.call-update) | async-done | bytes 8388624 | tf_op jit(solution)/shard_map/all_gather | solution.py:33
  166.0 0.0 copy-done
  166.0 14.6 %fusion.4 = f32[4096,1024]{1,0:T(8,128)} fusion(bf16[1024,4096]{1,0:T(8,128)(2,1)} %all-gather.2.cloned.1.call-done, bf16[1024,1024]{1,0:T(8,128)(2,1)S(1)} %copy-done), kind=kOutput, calls=%fused_computation.12 | convolution fusion | flops 8589934592 | bytes 27262976 | tf_op jit(solution)/shard_map/dot_general | solution.py:13
  180.6 0.0 reduce-scatter.2.cloned.1.call-update
  180.7 14.0 %all-reduce = (f32[1024]{0:T(1024)S(1)}, f32[1024]{0:T(1024)S(1)}) all-reduce(f32[1024]{0:T(1024)S(1)} %get-tuple-element.3, f32[1024]{0:T(1024)S(1)} %get-tuple-element.2), channel_id=1, replica_groups=mesh['cells'=8,'genes'=4] {'cells'}, use_global_device_ids=true, to_apply=%region_4.0 | all-reduce | flops 2048 | bytes 16384 | tf_op jit(solution)/shard_map/psum | solution.py:28
  194.7 13.2 %all_gather.10 = f32[4096]{0:T(1024)S(1)} all-gather(f32[1024]{0:T(1024)S(1)} %get-tuple-element.5), channel_id=1, replica_groups=mesh['cells'=8,'genes'=4] {'genes'}, dimensions={0}, use_global_device_ids=true | all-gather | bytes 20480 | tf_op jit(solution)/shard_map/all_gather | solution.py:30
  207.9 13.2 %all_gather.11 = f32[4096]{0:T(1024)S(1)} all-gather(f32[1024]{0:T(1024)S(1)} %get-tuple-element.4), channel_id=1, replica_groups=mesh['cells'=8,'genes'=4] {'genes'}, dimensions={0}, use_global_device_ids=true | all-gather | bytes 20480 | tf_op jit(solution)/shard_map/all_gather | solution.py:31
  221.1 0.1 dynamic_slice.12
  221.2 0.1 dynamic_slice.14
  221.3 73.9 %reduce-scatter.2.cloned.1.call-done = f32[512,1024]{1,0:T(8,128)} async-done(((f32[4096,1024]{1,0:T(8,128)}), f32[512,1024]{1,0:T(8,128)}) %reduce-scatter.2.cloned.1.call-update) | async-done | bytes 2097168 | tf_op jit(solution)/shard_map/reduce_scatter | solution.py:34
  295.2 3.8 %fusion.2 = (f32[512]{0:T(512)S(1)}, f32[512,1024]{1,0:T(8,128)}) fusion(f32[1024]{0:T(1024)S(1)} %dynamic_slice.15, f32[512]{0:T(512)S(1)} %dynamic_slice.14, f32[1024]{0:T(1024)S(1)} %dynamic_slice.13, f32[512]{0:T(512)S(1)} %dynamic_slice.12, f32[512,1024]{1,0:T(8,128)} %reduce-scatter.2.cloned.1.call-done, s32[1024]{0:T(1024)S(1)} %iota_add_fusion, ...), kind=kLoop, calls=%fused_computation.11 | loop fusion | flops 5766656 | bytes 4214784 | tf_op jit(solution)/shard_map/reduce_sum | solution.py:55
  299.0 12.2 %psum.23 = f32[512]{0:T(512)} all-reduce(f32[512]{0:T(512)S(1)} %get-tuple-element.6), channel_id=1, replica_groups=mesh['cells'=8,'genes'=4] {'genes'}, use_global_device_ids=true, to_apply=%region_6.7 | all-reduce | flops 512 | bytes 4096 | tf_op jit(solution)/shard_map/psum | solution.py:55
  (5 shorter events, 0.0 us)
Async XLA Ops:
  7.2 158.8 %all-gather.2.cloned.1.call-start = ((), (), s32[]{:S(2)}) async-start(), calls=%async_computation.1 | async-start | bytes 10485760 | tf_op jit(solution)/shard_map/all_gather | solution.py:33
  13.5 152.5 %copy-start = (bf16[1024,1024]{1,0:T(8,128)(2,1)S(1)}, bf16[1024,1024]{1,0:T(8,128)(2,1)}, u32[]{:S(2)}) copy-start(bf16[1024,1024]{1,0:T(8,128)(2,1)} %get-tuple-element.8) | copy-start | bytes 6291460
  13.5 281.7 %reduce-scatter.2.cloned.1.call-start = ((), (), s32[]{:S(2)}) async-start(), calls=%async_computation.2 | async-start | bytes 18874368 | tf_op jit(solution)/shard_map/reduce_scatter | solution.py:34
Sparse Core Ops, SparseCore 0:
  13.6 152.3 all-gather.1
  180.8 114.3 reduce-scatter.1
where the time goes:
time: 318 us
  waiting for transfers between devices  226 us (71%)
  blocking collectives  52.7 us (17%)
  matrix products  14.6 us (5%)
  between operations  14.1 us (4%)
  other arithmetic  10 us (3%)
    all_gather x1, waiting for transfers between devices, shards(): full_block = lax.all_gather(own_block, 'genes', axis=1, tiled=True)  152 us
    reduce_scatter x1, waiting for transfers between devices, shards(): lax.psum_scatter(cross_product(full_block, own_block), 'cells', scatter_d...  73.9 us
    dot_general x1, matrix products, cross_product(): lax.dot_general(left, right, (((0,), (0,)), ((), ())), preferred_element_...  14.6 us
    psum x1, blocking collectives, shards(): block_sums, block_squares = lax.psum((local_sums, local_squares), 'cells')  14 us
    all_gather x1, blocking collectives, shards(): lax.all_gather(block_sums, 'genes', axis=0, tiled=True)  13.2 us
    all_gather x1, blocking collectives, shards(): lax.all_gather(block_squares, 'genes', axis=0, tiled=True)  13.2 us
    psum x1, blocking collectives, shards(): connectivity = lax.psum(jnp.sum(adjacency, axis=1), 'genes')  12.2 us
  transfers between devices with their start and end apart: 2, of which 2 were waited for; matrix products, arithmetic and copies ran while one was open for 0% of the time, Pallas kernels for 0%

commit v1 on v0

--- a/solution.py
+++ b/solution.py
@@ -30,7 +30,9 @@
         lax.all_gather(block_sums, "genes", axis=0, tiled=True),
         lax.all_gather(block_squares, "genes", axis=0, tiled=True),
     )
-    full_block = lax.all_gather(own_block, "genes", axis=1, tiled=True)
+    full_block = jnp.concatenate(
+        lax.all_to_all(jnp.stack([own_block] * lax.axis_size("genes")), "genes", 0, 0), axis=1
+    )
     gram_tile = lax.psum_scatter(
         cross_product(full_block, own_block), "cells", scatter_dimension=0, tiled=True
     )

time: 318 us -> 358 us (1.13)
  blocking collectives: 52.7 us -> 241 us
  waiting for transfers between devices: 226 us -> 76.5 us
  local copies, waits for them, and re-layouts: 0.17 us -> 4.22 us
    all_to_all x0 -> x1, blocking collectives: none -> 189 us  [shards(): lax.all_to_all(jnp.stack([own_block] * lax.axis_size('genes')), 'genes',...]
    all_gather x1 -> x0, waiting for transfers between devices: 152 us -> none  [shards(): full_block = lax.all_gather(own_block, 'genes', axis=1, tiled=True)]
  transfers between devices with their start and end apart: 2 -> 1, of which waited for: 2 -> 1; matrix products, arithmetic and copies ran while one was open for 0% -> 0% of each run, Pallas kernels for 0% -> 0%
where the time goes in v1:
time: 358 us; the launch traced here: 357 us
  blocking collectives  241 us (67%)
  waiting for transfers between devices  76.5 us (21%)
  between operations  14.1 us (4%)
  matrix products  11.6 us (3%)
  other arithmetic  10 us (3%)
  local copies, waits for them, and re-layouts  4.22 us (1%)
    all_to_all x1, blocking collectives, shards(): lax.all_to_all(jnp.stack([own_block] * lax.axis_size('genes')), 'genes',...  189 us
    reduce_scatter x1, waiting for transfers between devices, shards(): lax.psum_scatter(cross_product(full_block, own_block), 'cells', scatter_d...  76.5 us
    all_gather x1, blocking collectives, shards(): lax.all_gather(block_sums, 'genes', axis=0, tiled=True)  13.2 us
    all_gather x1, blocking collectives, shards(): lax.all_gather(block_squares, 'genes', axis=0, tiled=True)  13.2 us
    psum x1, blocking collectives, shards(): block_sums, block_squares = lax.psum((local_sums, local_squares), 'cells')  12.8 us
    psum x1, blocking collectives, shards(): connectivity = lax.psum(jnp.sum(adjacency, axis=1), 'genes')  12.2 us
    dot_general x1, matrix products, cross_product(): lax.dot_general(left, right, (((0,), (0,)), ((), ())), preferred_element_...  11.6 us
  transfers between devices with their start and end apart: 1, of which 1 were waited for; matrix products, arithmetic and copies ran while one was open for 0% of the time, Pallas kernels for 0%

profile of v1, /device:TPU:0, one launch (start us, length us, event | category | flops | bytes accessed | tf_op | source)
XLA Modules:
  0.0 357.4 jit_solution(1155195627973683603)
XLA Ops:
  7.2 0.0 reduce-scatter.2.cloned.1.call-start
  7.2 0.7 convert_divide_fusion
  7.9 5.6 %convert_reduce_fusion = (f32[1024]{0:T(1024)S(1)}, f32[1024]{0:T(1024)S(1)}, bf16[1024,1024]{1,0:T(8,128)(2,1)}) fusion(f32[1024]{0:T(1024)S(1)} %convert_divide_fusion, s32[1024,1024]{1,0:T(8,128)} %param.2), kind=kLoop, calls=%fused_computation.1 | loop fusion | flops 7337984 | bytes 6303744 | tf_op jit(solution)/shard_map/reduce_sum | solution.py:26
  13.5 2.9 copy.5
  16.3 1.2 stack.2
  17.5 0.0 copy-start
  17.5 189.3 %all_to_all.5 = bf16[4,1024,1024]{1,2,0:T(8,128)(2,1)S(1)} all-to-all(bf16[4,1024,1024]{1,2,0:T(8,128)(2,1)S(1)} %stack.2), channel_id=1, replica_groups=mesh['cells'=8,'genes'=4] {'genes'}, dimensions={0} | all-to-all | bytes 16777216 | tf_op jit(solution)/shard_map/all_to_all | solution.py:34
  206.8 0.0 copy-done
  206.8 11.6 %fusion.4 = f32[4096,1024]{1,0:T(8,128)} fusion(bf16[1024,4096]{0,1:T(8,128)(2,1)S(1)} %bitcast.5, bf16[1024,1024]{1,0:T(8,128)(2,1)S(1)} %copy-done), kind=kOutput, calls=%fused_computation.12 | convolution fusion | flops 8589934592 | bytes 27262976 | tf_op jit(solution)/shard_map/dot_general | solution.py:13
  218.5 0.0 reduce-scatter.2.cloned.1.call-update
  218.5 12.8 %all-reduce = (f32[1024]{0:T(1024)S(1)}, f32[1024]{0:T(1024)S(1)}) all-reduce(f32[1024]{0:T(1024)S(1)} %get-tuple-element.3, f32[1024]{0:T(1024)S(1)} %get-tuple-element.2), channel_id=1, replica_groups=mesh['cells'=8,'genes'=4] {'cells'}, use_global_device_ids=true, to_apply=%region_4.0 | all-reduce | flops 2048 | bytes 16384 | tf_op jit(solution)/shard_map/psum | solution.py:28
  231.4 13.2 %all_gather.6 = f32[4096]{0:T(1024)S(1)} all-gather(f32[1024]{0:T(1024)S(1)} %get-tuple-element.5), channel_id=1, replica_groups=mesh['cells'=8,'genes'=4] {'genes'}, dimensions={0}, use_global_device_ids=true | all-gather | bytes 20480 | tf_op jit(solution)/shard_map/all_gather | solution.py:30
  244.6 13.2 %all_gather.7 = f32[4096]{0:T(1024)S(1)} all-gather(f32[1024]{0:T(1024)S(1)} %get-tuple-element.4), channel_id=1, replica_groups=mesh['cells'=8,'genes'=4] {'genes'}, dimensions={0}, use_global_device_ids=true | all-gather | bytes 20480 | tf_op jit(solution)/shard_map/all_gather | solution.py:31
  257.8 0.1 dynamic_slice.12
  257.9 0.1 dynamic_slice.14
  258.0 76.5 %reduce-scatter.2.cloned.1.call-done = f32[512,1024]{1,0:T(8,128)} async-done(((f32[4096,1024]{1,0:T(8,128)}), f32[512,1024]{1,0:T(8,128)}) %reduce-scatter.2.cloned.1.call-update) | async-done | bytes 2097168 | tf_op jit(solution)/shard_map/reduce_scatter | solution.py:36
  334.5 3.8 %fusion.2 = (f32[512]{0:T(512)S(1)}, f32[512,1024]{1,0:T(8,128)}) fusion(f32[1024]{0:T(1024)S(1)} %dynamic_slice.15, f32[512]{0:T(512)S(1)} %dynamic_slice.14, f32[1024]{0:T(1024)S(1)} %dynamic_slice.13, f32[512]{0:T(512)S(1)} %dynamic_slice.12, f32[512,1024]{1,0:T(8,128)} %reduce-scatter.2.cloned.1.call-done, s32[1024]{0:T(1024)S(1)} %iota_add_fusion, ...), kind=kLoop, calls=%fused_computation.11 | loop fusion | flops 5766656 | bytes 4214784 | tf_op jit(solution)/shard_map/reduce_sum | solution.py:57
  338.3 12.2 %psum.23 = f32[512]{0:T(512)} all-reduce(f32[512]{0:T(512)S(1)} %get-tuple-element.6), channel_id=1, replica_groups=mesh['cells'=8,'genes'=4] {'genes'}, use_global_device_ids=true, to_apply=%region_6.7 | all-reduce | flops 512 | bytes 4096 | tf_op jit(solution)/shard_map/psum | solution.py:57
  (5 shorter events, 0.0 us)
Async XLA Ops:
  7.2 327.4 %reduce-scatter.2.cloned.1.call-start = ((), (), s32[]{:S(2)}) async-start(), calls=%async_computation.2 | async-start | bytes 18874368 | tf_op jit(solution)/shard_map/reduce_scatter | solution.py:36
  17.5 189.3 %copy-start = (bf16[1024,1024]{1,0:T(8,128)(2,1)S(1)}, bf16[1024,1024]{1,0:T(8,128)(2,1)}, u32[]{:S(2)}) copy-start(bf16[1024,1024]{1,0:T(8,128)(2,1)} %get-tuple-element.8) | copy-start | bytes 6291460
Sparse Core Ops, SparseCore 0:
  218.6 115.8 reduce-scatter.1
